TPU v7x, 32 devices: a whole 2x2x4 slice. The times are simulated.
32 devices in a mesh: dom: 4 (over z), grp: 8 (over y, x, core).
Axes of the slice: x: 2, y: 2, z: 4, core: 2. Of those that a mesh axis runs over, the one named last changes fastest.
Arguments:
- master_rows: bfloat16 [8, 512, 512], P('grp', 'dom'), may hold values from -6 to 6
- cotangent: bfloat16 [8, 512, 512], P('grp', 'dom'), may hold values from -6 to 6
- relation_weight: bfloat16 [4, 512, 512], replicated, may hold values from -0.125 to 0.125
- self_weight: bfloat16 [512, 512], replicated, may hold values from -0.25 to 0.25
- edge_source: int32 [8, 8192], P('grp', 'dom'), may hold values from 0 to 191
- edge_target: int32 [8, 8192], P('grp', 'dom'), may hold values from 0 to 191
- edge_relation: int32 [8, 8192], P('grp', 'dom'), may hold values from 0 to 3
- send_rows: int32 [8, 256], P('grp', 'dom'), may hold values from 0 to 127
- send_counts: int32 [8, 16], P('grp', 'dom'), may hold values from 4 to 16, as said below
Outputs:
- activation: bfloat16 [8, 512, 512], P('grp', 'dom')
- input_grad: bfloat16 [8, 512, 512], P('grp', 'dom')
- weight_grads: float32 [5, 512, 512], P(None, 'grp')
Inputs may be any that keep to these rules, and one draw needn't show every extreme that they name: `send_counts`: on every device the count for some peer is exactly 16.
All inputs are finite; a program needn't handle non-finite values.
Results may differ from a plain program's by a relative error of at most 0.0061.
Values may be sent and summed in bfloat16 or wider, within the bound.
No kernel may reach another device: no remote copies, remote signals or barrier semaphores. Data moves between devices by JAX's collectives and lax.ppermute only.
A program may use at most 64 MiB of HBM per device.

v0:
```python
import jax
import jax.numpy as jnp
from jax import lax
from jax.sharding import PartitionSpec as P


def pull_rows(table, send_rows, valid):
    domains = lax.axis_size("dom")
    width = table.shape[1]
    picked = table[send_rows]
    picked = jnp.where(valid[:, None], picked, jnp.zeros_like(picked))
    moved = lax.all_to_all(
        picked.reshape(domains, -1, width), "dom", split_axis=0, concat_axis=0, tiled=True
    )
    return jnp.concatenate([table, moved.reshape(-1, width)], axis=0)


def push_rows(mirror_part, placement, own):
    domains = lax.axis_size("dom")
    width = own.shape[1]
    moved = lax.all_to_all(
        mirror_part.reshape(domains, -1, width), "dom", split_axis=0, concat_axis=0, tiled=True
    )
    return own + jnp.dot(placement, moved.reshape(-1, width), preferred_element_type=jnp.float32)


def edge_counts(sources, targets, relation, relations, local_rows):
    flat_index = (relation * local_rows + targets) * local_rows + sources
    ones = jnp.ones(sources.shape, jnp.float32)
    counted = jax.ops.segment_sum(
        ones, flat_index, num_segments=relations * local_rows * local_rows
    )
    return counted.reshape(relations, local_rows, local_rows).astype(jnp.bfloat16)


def per_device(
    master_rows,
    cotangent,
    relation_weight,
    self_weight,
    edge_source,
    edge_target,
    edge_relation,
    send_rows,
    send_counts,
):
    masters = master_rows[0]
    cotan = cotangent[0]
    sources = edge_source[0]
    targets = edge_target[0]
    relation = edge_relation[0]
    slots = send_rows[0]
    counts = send_counts[0]
    domains = lax.axis_size("dom")
    relations = relation_weight.shape[0]
    master_count = masters.shape[0]
    capacity = slots.shape[0] // domains
    valid = (jnp.arange(capacity)[None, :] < counts[:, None]).reshape(-1)
    placement = ((slots[None, :] == jnp.arange(master_count)[:, None]) & valid[None, :]).astype(
        jnp.bfloat16
    )
    table = pull_rows(masters, slots, valid)
    local_rows = table.shape[0]
    adjacency = edge_counts(sources, targets, relation, relations, local_rows)
    aggregated = jnp.einsum(
        "rij,jd->rid", adjacency, table, preferred_element_type=jnp.float32
    ).astype(jnp.bfloat16)
    partial_value = jnp.einsum(
        "rnd,rde->ne", aggregated, relation_weight, preferred_element_type=jnp.float32
    )
    own = partial_value[:master_count] + jnp.dot(
        masters, self_weight, preferred_element_type=jnp.float32
    )
    z_value = push_rows(partial_value[master_count:].astype(jnp.bfloat16), placement, own)
    activation = jax.nn.silu(z_value).astype(jnp.bfloat16)
    sigmoid_z = jax.nn.sigmoid(z_value)
    grad_z = (cotan.astype(jnp.float32) * sigmoid_z * (1.0 + z_value * (1.0 - sigmoid_z))).astype(
        jnp.bfloat16
    )
    grad_table = pull_rows(grad_z, slots, valid)
    relation_grad = jnp.einsum(
        "rnd,ne->rde", aggregated, grad_table, preferred_element_type=jnp.float32
    )
    self_grad = jnp.dot(masters.T, grad_z, preferred_element_type=jnp.float32)
    local_grads = jnp.concatenate([relation_grad, self_grad[None]], axis=0)
    group_part = lax.psum_scatter(local_grads, "grp", scatter_dimension=1, tiled=True)
    weight_grads = lax.psum(group_part, "dom")
    back = jnp.einsum(
        "rij,id->rjd", adjacency, grad_table, preferred_element_type=jnp.float32
    ).astype(jnp.bfloat16)
    back_partial = jnp.einsum(
        "rne,rde->nd", back, relation_weight, preferred_element_type=jnp.float32
    )
    back_own = back_partial[:master_count] + jnp.dot(
        grad_z, self_weight.T, preferred_element_type=jnp.float32
    )
    input_grad = push_rows(back_partial[master_count:].astype(jnp.bfloat16), placement, back_own)
    return (activation[None], input_grad.astype(jnp.bfloat16)[None], weight_grads)


def solution(mesh):
    return jax.shard_map(
        per_device,
        mesh=mesh,
        in_specs=(
            P("grp", "dom", None),
            P("grp", "dom", None),
            P(),
            P(),
            P("grp", "dom"),
            P("grp", "dom"),
            P("grp", "dom"),
            P("grp", "dom"),
            P("grp", "dom"),
        ),
        out_specs=(P("grp", "dom", None), P("grp", "dom", None), P(None, "grp", None)),
        check_vma=False,
    )
```

profile of v0, /device:TPU:0, one launch (start us, length us, event | category | flops | bytes accessed | tf_op | source)
XLA Modules:
  0.0 171.5 jit_solution(12031938624284277153)
XLA Ops:
  7.2 0.9 iota_compare_fusion.1
  8.1 0.7 fusion.23
  8.8 1.6 gather_fusion
  10.4 0.7 broadcast_select_fusion.1
  11.1 6.3 %all-to-all-start = ((bf16[4,16,512]{2,1,0:T(8,128)(2,1)}), bf16[4,16,512]{2,1,0:T(8,128)(2,1)}, u32[]{:S(2)}, u32[]{:S(2)}) async-start(bf16[4,16,512]{2,1,0:T(8,128)(2,1)} %broadcast_select_fusion.1), calls=%async_computation | async-start | bytes 131072 | tf_op jit(solution)/shard_map/all_to_all | solution.py:12
  17.4 0.7 multiply_add_fusion
  18.2 11.4 %scatter_custom_fusion = f32[147456]{0:T(1024)S(1)} fusion(s32[2048]{0:T(1024)S(1)} %bitcast.64, f32[2048]{0:T(1024)S(1)} %broadcast.65, f32[]{:T(128)} %constant.6.clone.1), kind=kCustom, calls=%fused_computation.16 | custom fusion | flops 2048 | bytes 589828 | tf_op jit(solution)/shard_map/scatter-add | solution.py:30
  29.6 0.3 convert_element_type.31
  29.9 1.2 convolution_convert_fusion.1
  31.2 0.6 convolution_bitcast_fusion.1
  31.8 0.7 copy-done.3
  32.5 0.6 slice.31
  33.1 5.1 %all-to-all-start.1 = ((bf16[4,16,512]{2,1,0:T(8,128)(2,1)}), bf16[4,16,512]{2,1,0:T(8,128)(2,1)S(1)}, u32[]{:S(2)}, u32[]{:S(2)}) async-start(bf16[4,16,512]{2,1,0:T(8,128)(2,1)} %bitcast.10), calls=%async_computation.1 | async-start | bytes 131072 | tf_op jit(solution)/shard_map/all_to_all | solution.py:21
  38.2 0.1 lt.42
  38.3 5.7 %all-to-all-done.1 = bf16[4,16,512]{2,1,0:T(8,128)(2,1)S(1)} async-done(((bf16[4,16,512]{2,1,0:T(8,128)(2,1)}), bf16[4,16,512]{2,1,0:T(8,128)(2,1)S(1)}, u32[]{:S(2)}, u32[]{:S(2)}) %all-to-all-start.1) | async-done | bytes 65568 | tf_op jit(solution)/shard_map/all_to_all | solution.py:21
  44.0 0.2 fusion.17
  44.1 2.2 %fusion.9 = (bf16[128,512]{1,0:T(8,128)(2,1)S(1)}, bf16[1,128,512]{2,1,0:T(8,128)(2,1)}) fusion(bf16[1,128,512]{2,1,0:T(8,128)(2,1)} %param.10, f32[128,512]{1,0:T(8,128)S(1)} %fusion.17, bf16[512,512]{1,0:T(8,128)(2,1)} %param.12, bf16[1,128,512]{2,1,0:T(8,128)(2,1)S(1)} %copy-done.1, f32[192,512]{1,0:T(8,128)} %copy-done.3), kind=kOutput, calls=%fused_computation.20 | convolution fusion | flops 68026368 | bytes 1572864 | tf_op jit(solution)/shard_map/dot_general | solution.py:71
  46.3 1.3 gather_fusion.1
  47.6 1.5 broadcast_select_fusion
  49.2 3.9 %all-to-all-start.2 = ((bf16[4,16,512]{2,1,0:T(8,128)(2,1)}), bf16[4,16,512]{2,1,0:T(8,128)(2,1)}, u32[]{:S(2)}, u32[]{:S(2)}) async-start(bf16[4,16,512]{2,1,0:T(8,128)(2,1)} %broadcast_select_fusion), calls=%async_computation.2 | async-start | bytes 131072 | tf_op jit(solution)/shard_map/all_to_all | solution.py:12
  53.1 1.3 convolution_bitcast_fusion
  54.5 4.4 %all-to-all-done.2 = bf16[4,16,512]{2,1,0:T(8,128)(2,1)} async-done(((bf16[4,16,512]{2,1,0:T(8,128)(2,1)}), bf16[4,16,512]{2,1,0:T(8,128)(2,1)}, u32[]{:S(2)}, u32[]{:S(2)}) %all-to-all-start.2) | async-done | bytes 65568 | tf_op jit(solution)/shard_map/all_to_all | solution.py:12
  58.9 1.7 fusion.13
  60.6 2.9 %pad_maximum_fusion = f32[5,512,512]{2,1,0:T(8,128)} fusion(f32[1,512,512]{2,1,0:T(8,128)S(1)} %copy-done.2, f32[4,512,512]{2,1,0:T(8,128)S(1)} %fusion.13), kind=kLoop, calls=%fused_computation.3 | loop fusion | flops 1310720 | bytes 10485760 | tf_op jit(solution)/shard_map/concatenate | solution.py:85
  63.5 55.1 %reduce-scatter.2.cloned.1.call-done = f32[5,64,512]{2,1,0:T(8,128)} async-done(((f32[5,512,512]{2,1,0:T(8,128)}), f32[5,64,512]{2,1,0:T(8,128)}) %reduce-scatter.2.cloned.1.call-update) | async-done | bytes 655376 | tf_op jit(solution)/shard_map/reduce_scatter | solution.py:86
  118.7 2.7 %fusion.1 = f32[192,512]{1,0:T(8,128)} fusion(bf16[4,512,512]{2,1,0:T(8,128)(2,1)S(1)} %copy-done, bf16[4,192,192]{2,1,0:T(8,128)(2,1)S(1)} %convert_element_type.31, bf16[64,512]{1,0:T(8,128)(2,1)} %bitcast.15, bf16[128,512]{1,0:T(8,128)(2,1)S(1)} %get-tuple-element.3), kind=kOutput, calls=%fused_computation.8 | convolution fusion | flops 554434560 | bytes 2981888 | tf_op jit(solution)/shard_map/rne,rde->nd/dot_general | solution.py:91
  121.4 0.9 slice.30
  122.3 11.1 %all_to_all.20 = bf16[4,16,512]{2,1,0:T(8,128)(2,1)S(1)} all-to-all(bf16[4,16,512]{2,1,0:T(8,128)(2,1)S(1)} %bitcast.61), channel_id=1, replica_groups=mesh['dom'=4,'grp'=8] {'dom'}, dimensions={0} | all-to-all | bytes 131072 | tf_op jit(solution)/shard_map/all_to_all | solution.py:21
  133.4 0.2 fusion.15
  133.6 1.9 %fusion.5 = bf16[1,128,512]{2,1,0:T(8,128)(2,1)} fusion(f32[128,512]{1,0:T(8,128)S(1)} %fusion.15, bf16[128,512]{1,0:T(8,128)(2,1)S(1)} %get-tuple-element.3, bf16[512,512]{1,0:T(8,128)(2,1)S(1)} %copy-done.4, f32[192,512]{1,0:T(8,128)} %fusion.1), kind=kOutput, calls=%fused_computation.15 | convolution fusion | flops 67305472 | bytes 1310720 | tf_op jit(solution)/shard_map/dot_general | solution.py:94
  135.5 27.2 %all-reduce.2.cloned.1.call-done = f32[5,64,512]{2,1,0:T(8,128)} async-done(((f32[5,64,512]{2,1,0:T(8,128)}), f32[5,64,512]{2,1,0:T(8,128)}) %all-reduce.2.cloned.1.call-update) | async-done | bytes 655376 | tf_op jit(solution)/shard_map/psum | solution.py:87
  162.7 2.0 %copy.15 = f32[5,64,512]{2,1,0:T(8,128)} copy(f32[5,64,512]{2,1,0:T(8,128)} %all-reduce.2.cloned.1.call-done) | data formatting | bytes 1310720
  (19 shorter events, 0.2 us)
Async XLA Ops:
  7.2 24.0 %copy-start = (bf16[4,512,512]{2,1,0:T(8,128)(2,1)S(1)}, bf16[4,512,512]{2,1,0:T(8,128)(2,1)}, u32[]{:S(2)}) copy-start(bf16[4,512,512]{2,1,0:T(8,128)(2,1)} %param.11) | copy-start | bytes 6291460
  7.2 22.8 %copy-start.1 = (bf16[1,128,512]{2,1,0:T(8,128)(2,1)S(1)}, bf16[1,128,512]{2,1,0:T(8,128)(2,1)}, u32[]{:S(2)}) copy-start(bf16[1,128,512]{2,1,0:T(8,128)(2,1)} %param.9) | copy-start | bytes 393220
  11.1 18.8 %all-to-all-start = ((bf16[4,16,512]{2,1,0:T(8,128)(2,1)}), bf16[4,16,512]{2,1,0:T(8,128)(2,1)}, u32[]{:S(2)}, u32[]{:S(2)}) async-start(bf16[4,16,512]{2,1,0:T(8,128)(2,1)} %broadcast_select_fusion.1), calls=%async_computation | async-start | bytes 131072 | tf_op jit(solution)/shard_map/all_to_all | solution.py:12
  31.2 12.8 %copy-start.5 = (s32[1,64]{1,0:T(1,128)S(1)}, s32[1,64]{1,0:T(1,128)}, u32[]{:S(2)}) copy-start(s32[1,64]{1,0:T(1,128)} %param.16) | copy-start | bytes 772
  31.7 0.7 copy-start.3
  33.1 10.8 %all-to-all-start.1 = ((bf16[4,16,512]{2,1,0:T(8,128)(2,1)}), bf16[4,16,512]{2,1,0:T(8,128)(2,1)S(1)}, u32[]{:S(2)}, u32[]{:S(2)}) async-start(bf16[4,16,512]{2,1,0:T(8,128)(2,1)} %bitcast.10), calls=%async_computation.1 | async-start | bytes 131072 | tf_op jit(solution)/shard_map/all_to_all | solution.py:21
  49.2 9.7 %all-to-all-start.2 = ((bf16[4,16,512]{2,1,0:T(8,128)(2,1)}), bf16[4,16,512]{2,1,0:T(8,128)(2,1)}, u32[]{:S(2)}, u32[]{:S(2)}) async-start(bf16[4,16,512]{2,1,0:T(8,128)(2,1)} %broadcast_select_fusion), calls=%async_computation.2 | async-start | bytes 131072 | tf_op jit(solution)/shard_map/all_to_all | solution.py:12
  53.1 65.5 %reduce-scatter.2.cloned.1.call-start = ((), (), s32[]{:S(2)}) async-start(), calls=%async_computation.5 | async-start | bytes 5898240 | tf_op jit(solution)/shard_map/reduce_scatter | solution.py:86
  58.9 1.7 copy-start.2
  63.5 99.2 %all-reduce.2.cloned.1.call-start = ((), (), s32[]{:S(2)}) async-start(), calls=%async_computation.6 | async-start | bytes 1310720 | tf_op jit(solution)/shard_map/psum | solution.py:87
  118.7 14.9 %copy-start.4 = (bf16[512,512]{1,0:T(8,128)(2,1)S(1)}, bf16[512,512]{1,0:T(8,128)(2,1)}, u32[]{:S(2)}) copy-start(bf16[512,512]{1,0:T(8,128)(2,1)} %param.12) | copy-start | bytes 1572868
Sparse Core Ops, SparseCore 0:
  63.6 54.9 reduce-scatter.1
  121.0 41.6 all-reduce.1
where the time goes:
time: 172 us; the launch traced here: 171 us
  waiting for transfers between devices  92.4 us (54%)
  other arithmetic  18.9 us (11%)
  starting transfers between devices  15.4 us (9%)
  between operations  14.2 us (8%)
  matrix products  11.9 us (7%)
  blocking collectives  11.1 us (6%)
  local copies, waits for them, and re-layouts  7.62 us (4%)
    reduce_scatter x1, waiting for transfers between devices, per_device(): lax.psum_scatter(local_grads, 'grp', scatter_dimension=1, tiled=True)  55.1 us
    psum x1, waiting for transfers between devices, per_device(): weight_grads = lax.psum(group_part, 'dom')  27.2 us
    scatter-add x1, other arithmetic, edge_counts(): jax.ops.segment_sum(ones, flat_index, num_segments=relations * local_rows...  11.4 us
    all_to_all x1, blocking collectives, push_rows(): lax.all_to_all(mirror_part.reshape(domains, -1, width), 'dom', split_axis...  11.1 us
    all_to_all x2, starting transfers between devices, pull_rows(): lax.all_to_all(picked.reshape(domains, -1, width), 'dom', split_axis=0, c...  10.2 us
    all_to_all x1, waiting for transfers between devices, push_rows(): lax.all_to_all(mirror_part.reshape(domains, -1, width), 'dom', split_axis...  5.66 us
    all_to_all x1, starting transfers between devices, push_rows(): lax.all_to_all(mirror_part.reshape(domains, -1, width), 'dom', split_axis...  5.08 us
    all_to_all x2, waiting for transfers between devices, pull_rows(): lax.all_to_all(picked.reshape(domains, -1, width), 'dom', split_axis=0, c...  4.44 us
  transfers between devices with their start and end apart: 5, of which 4 were waited for; matrix products, arithmetic and copies ran while one was open for 11% of the time, Pallas kernels for 0%

commit v1 on v0

--- a/solution.py
+++ b/solution.py
@@ -84,7 +84,11 @@
     self_grad = jnp.dot(masters.T, grad_z, preferred_element_type=jnp.float32)
     local_grads = jnp.concatenate([relation_grad, self_grad[None]], axis=0)
     group_part = lax.psum_scatter(local_grads, "grp", scatter_dimension=1, tiled=True)
-    weight_grads = lax.psum(group_part, "dom")
+    weight_grads = group_part
+    for hop in (1, 2):
+        weight_grads = weight_grads + lax.ppermute(
+            weight_grads, "dom", [(dev, dev ^ hop) for dev in range(4)]
+        )
     back = jnp.einsum(
         "rij,id->rjd", adjacency, grad_table, preferred_element_type=jnp.float32
     ).astype(jnp.bfloat16)

time: 172 us -> 181 us (1.052)
  blocking collectives: 11.1 us -> 25.8 us
  waiting for transfers between devices: 92.4 us -> 80.3 us
  starting transfers between devices: 15.4 us -> 19.3 us
  other arithmetic: 18.9 us -> 22.1 us
    psum x1 -> x0, waiting for transfers between devices: 27.2 us -> none  [per_device(): weight_grads = lax.psum(group_part, 'dom')]
    ppermute x0 -> x2, waiting for transfers between devices: none -> 15 us  [per_device(): lax.ppermute(weight_grads, 'dom', [(dev, dev ^ hop) for dev in range(4)])]
    all_to_all x1, blocking collectives: 11.1 us -> 25.8 us  [push_rows(): lax.all_to_all(mirror_part.reshape(domains, -1, width), 'dom', split_axis...]
    ppermute x0 -> x2, starting transfers between devices: none -> 3.97 us  [per_device(): lax.ppermute(weight_grads, 'dom', [(dev, dev ^ hop) for dev in range(4)])]
    add x0 -> x2, other arithmetic: none -> 3.22 us  [per_device(): weight_grads + lax.ppermute(weight_grads, 'dom', [(dev, dev ^ hop) for de...]
  transfers between devices with their start and end apart: 5 -> 6, of which waited for: 4 -> 4; matrix products, arithmetic and copies ran while one was open for 11% -> 11% of each run, Pallas kernels for 0% -> 0%
where the time goes in v1:
time: 181 us; the launch traced here: 180 us
  waiting for transfers between devices  80.3 us (44%)
  blocking collectives  25.8 us (14%)
  other arithmetic  22.1 us (12%)
  starting transfers between devices  19.3 us (11%)
  between operations  14.2 us (8%)
  matrix products  11.9 us (7%)
  local copies, waits for them, and re-layouts  6.25 us (3%)
    reduce_scatter x1, waiting for transfers between devices, per_device(): lax.psum_scatter(local_grads, 'grp', scatter_dimension=1, tiled=True)  55.1 us
    all_to_all x1, blocking collectives, push_rows(): lax.all_to_all(mirror_part.reshape(domains, -1, width), 'dom', split_axis...  25.8 us
    ppermute x2, waiting for transfers between devices, per_device(): lax.ppermute(weight_grads, 'dom', [(dev, dev ^ hop) for dev in range(4)])  15 us
    scatter-add x1, other arithmetic, edge_counts(): jax.ops.segment_sum(ones, flat_index, num_segments=relations * local_rows...  11.4 us
    all_to_all x2, starting transfers between devices, pull_rows(): lax.all_to_all(picked.reshape(domains, -1, width), 'dom', split_axis=0, c...  10.2 us
    all_to_all x1, waiting for transfers between devices, push_rows(): lax.all_to_all(mirror_part.reshape(domains, -1, width), 'dom', split_axis...  5.66 us
    all_to_all x1, starting transfers between devices, push_rows(): lax.all_to_all(mirror_part.reshape(domains, -1, width), 'dom', split_axis...  5.09 us
    all_to_all x2, waiting for transfers between devices, pull_rows(): lax.all_to_all(picked.reshape(domains, -1, width), 'dom', split_axis=0, c...  4.44 us
  transfers between devices with their start and end apart: 6, of which 4 were waited for; matrix products, arithmetic and copies ran while one was open for 11% of the time, Pallas kernels for 0%

profile of v1, /device:TPU:0, one launch (start us, length us, event | category | flops | bytes accessed | tf_op | source)
XLA Modules:
  0.0 179.9 jit_solution(5536767361576202314)
XLA Ops:
  7.2 0.9 iota_compare_fusion.1
  8.1 0.7 fusion.23
  8.8 1.6 gather_fusion
  10.4 0.7 broadcast_select_fusion.1
  11.1 6.3 %all-to-all-start = ((bf16[4,16,512]{2,1,0:T(8,128)(2,1)}), bf16[4,16,512]{2,1,0:T(8,128)(2,1)S(1)}, u32[]{:S(2)}, u32[]{:S(2)}) async-start(bf16[4,16,512]{2,1,0:T(8,128)(2,1)} %broadcast_select_fusion.1), calls=%async_computation | async-start | bytes 131072 | tf_op jit(solution)/shard_map/all_to_all | solution.py:12
  17.4 0.7 multiply_add_fusion
  18.2 11.4 %scatter_custom_fusion = f32[147456]{0:T(1024)S(1)} fusion(s32[2048]{0:T(1024)S(1)} %bitcast.65, f32[2048]{0:T(1024)S(1)} %broadcast.65, f32[]{:T(128)} %constant.6.clone.1), kind=kCustom, calls=%fused_computation.16 | custom fusion | flops 2048 | bytes 589828 | tf_op jit(solution)/shard_map/scatter-add | solution.py:30
  29.9 0.6 copy-done.4
  30.6 1.2 convolution_convert_fusion.1
  31.8 0.6 convolution_bitcast_fusion.1
  32.4 0.7 copy-done.3
  33.1 0.6 slice.31
  33.8 5.1 %all-to-all-start.1 = ((bf16[4,16,512]{2,1,0:T(8,128)(2,1)}), bf16[4,16,512]{2,1,0:T(8,128)(2,1)S(1)}, u32[]{:S(2)}, u32[]{:S(2)}) async-start(bf16[4,16,512]{2,1,0:T(8,128)(2,1)} %bitcast.10), calls=%async_computation.1 | async-start | bytes 131072 | tf_op jit(solution)/shard_map/all_to_all | solution.py:21
  38.9 5.7 %all-to-all-done.1 = bf16[4,16,512]{2,1,0:T(8,128)(2,1)S(1)} async-done(((bf16[4,16,512]{2,1,0:T(8,128)(2,1)}), bf16[4,16,512]{2,1,0:T(8,128)(2,1)S(1)}, u32[]{:S(2)}, u32[]{:S(2)}) %all-to-all-start.1) | async-done | bytes 65568 | tf_op jit(solution)/shard_map/all_to_all | solution.py:21
  44.8 2.2 %fusion.9 = (bf16[128,512]{1,0:T(8,128)(2,1)S(1)}, bf16[1,128,512]{2,1,0:T(8,128)(2,1)}) fusion(bf16[1,128,512]{2,1,0:T(8,128)(2,1)} %param.10, f32[128,512]{1,0:T(8,128)S(1)} %fusion.17, bf16[512,512]{1,0:T(8,128)(2,1)} %param.12, bf16[1,128,512]{2,1,0:T(8,128)(2,1)S(1)} %copy-done.1, f32[192,512]{1,0:T(8,128)} %copy-done.3), kind=kOutput, calls=%fused_computation.20 | convolution fusion | flops 68026368 | bytes 1572864 | tf_op jit(solution)/shard_map/dot_general | solution.py:71
  46.9 1.3 gather_fusion.1
  48.3 1.5 broadcast_select_fusion
  49.8 3.9 %all-to-all-start.2 = ((bf16[4,16,512]{2,1,0:T(8,128)(2,1)}), bf16[4,16,512]{2,1,0:T(8,128)(2,1)}, u32[]{:S(2)}, u32[]{:S(2)}) async-start(bf16[4,16,512]{2,1,0:T(8,128)(2,1)} %broadcast_select_fusion), calls=%async_computation.2 | async-start | bytes 131072 | tf_op jit(solution)/shard_map/all_to_all | solution.py:12
  53.8 1.3 convolution_bitcast_fusion
  55.1 4.4 %all-to-all-done.2 = bf16[4,16,512]{2,1,0:T(8,128)(2,1)} async-done(((bf16[4,16,512]{2,1,0:T(8,128)(2,1)}), bf16[4,16,512]{2,1,0:T(8,128)(2,1)}, u32[]{:S(2)}, u32[]{:S(2)}) %all-to-all-start.2) | async-done | bytes 65568 | tf_op jit(solution)/shard_map/all_to_all | solution.py:12
  59.5 1.7 fusion.13
  61.2 2.9 %pad_maximum_fusion = f32[5,512,512]{2,1,0:T(8,128)} fusion(f32[1,512,512]{2,1,0:T(8,128)S(1)} %copy-done.2, f32[4,512,512]{2,1,0:T(8,128)S(1)} %fusion.13), kind=kLoop, calls=%fused_computation.3 | loop fusion | flops 1310720 | bytes 10485760 | tf_op jit(solution)/shard_map/concatenate | solution.py:85
  64.1 55.1 %reduce-scatter.2.cloned.1.call-done = f32[5,64,512]{2,1,0:T(8,128)} async-done(((f32[5,512,512]{2,1,0:T(8,128)}), f32[5,64,512]{2,1,0:T(8,128)}) %reduce-scatter.2.cloned.1.call-update) | async-done | bytes 655376 | tf_op jit(solution)/shard_map/reduce_scatter | solution.py:86
  119.2 1.5 collective-permute-start
  120.7 15.0 %collective-permute-done = f32[5,64,512]{2,1,0:T(8,128)S(1)} collective-permute-done((f32[5,64,512]{2,1,0:T(8,128)}, f32[5,64,512]{2,1,0:T(8,128)S(1)}, u32[]{:S(2)}, u32[]{:S(2)}) %collective-permute-start) | collective-permute-done | bytes 655392 | tf_op jit(solution)/shard_map/ppermute | solution.py:89
  135.8 1.2 add.75
  137.0 2.5 %collective-permute-start.1 = (f32[5,64,512]{2,1,0:T(8,128)S(1)}, f32[5,64,512]{2,1,0:T(8,128)}, u32[]{:S(2)}, u32[]{:S(2)}) collective-permute-start(f32[5,64,512]{2,1,0:T(8,128)S(1)} %add.75), channel_id=1, source_target_pairs={{0,16},{8,24},{16,0},{24,8},{1,17},{9,25},{17,1},{25,9},{2,18},{10... | collective-permute-start | bytes 1966088 | tf_op jit(solution)/shard_map/ppermute | solution.py:89
  139.4 2.6 %fusion.1 = f32[192,512]{1,0:T(8,128)} fusion(bf16[4,512,512]{2,1,0:T(8,128)(2,1)S(1)} %copy-done, bf16[4,192,192]{2,1,0:T(8,128)(2,1)S(1)} %convert_element_type.31, bf16[64,512]{1,0:T(8,128)(2,1)} %bitcast.15, bf16[128,512]{1,0:T(8,128)(2,1)S(1)} %get-tuple-element.3), kind=kOutput, calls=%fused_computation.8 | convolution fusion | flops 554434560 | bytes 2981888 | tf_op jit(solution)/shard_map/rne,rde->nd/dot_general | solution.py:95
  142.1 0.9 slice.30
  143.0 25.8 %all_to_all.20 = bf16[4,16,512]{2,1,0:T(8,128)(2,1)S(1)} all-to-all(bf16[4,16,512]{2,1,0:T(8,128)(2,1)S(1)} %bitcast.61), channel_id=1, replica_groups=mesh['dom'=4,'grp'=8] {'dom'}, dimensions={0} | all-to-all | bytes 131072 | tf_op jit(solution)/shard_map/all_to_all | solution.py:21
  169.0 2.1 %fusion.5 = bf16[1,128,512]{2,1,0:T(8,128)(2,1)} fusion(f32[128,512]{1,0:T(8,128)S(1)} %fusion.15, bf16[128,512]{1,0:T(8,128)(2,1)S(1)} %get-tuple-element.3, bf16[512,512]{1,0:T(8,128)(2,1)} %param.12, f32[192,512]{1,0:T(8,128)} %fusion.1), kind=kOutput, calls=%fused_computation.15 | convolution fusion | flops 67305472 | bytes 1310720 | tf_op jit(solution)/shard_map/dot_general | solution.py:98
  171.1 2.0 %add.76 = f32[5,64,512]{2,1,0:T(8,128)} add(f32[5,64,512]{2,1,0:T(8,128)S(1)} %add.75, f32[5,64,512]{2,1,0:T(8,128)} %collective-permute-done.1) | non-fusion elementwise | flops 163840 | bytes 1966080 | tf_op jit(solution)/shard_map/add | solution.py:89
  (21 shorter events, 0.8 us)
Async XLA Ops:
  7.2 24.6 %copy-start = (bf16[4,512,512]{2,1,0:T(8,128)(2,1)S(1)}, bf16[4,512,512]{2,1,0:T(8,128)(2,1)}, u32[]{:S(2)}) copy-start(bf16[4,512,512]{2,1,0:T(8,128)(2,1)} %param.11) | copy-start | bytes 6291460
  7.2 23.4 %copy-start.1 = (bf16[1,128,512]{2,1,0:T(8,128)(2,1)S(1)}, bf16[1,128,512]{2,1,0:T(8,128)(2,1)}, u32[]{:S(2)}) copy-start(bf16[1,128,512]{2,1,0:T(8,128)(2,1)} %param.9) | copy-start | bytes 393220
  11.1 18.8 %all-to-all-start = ((bf16[4,16,512]{2,1,0:T(8,128)(2,1)}), bf16[4,16,512]{2,1,0:T(8,128)(2,1)S(1)}, u32[]{:S(2)}, u32[]{:S(2)}) async-start(bf16[4,16,512]{2,1,0:T(8,128)(2,1)} %broadcast_select_fusion.1), calls=%async_computation | async-start | bytes 131072 | tf_op jit(solution)/shard_map/all_to_all | solution.py:12
  29.9 0.6 copy-start.4
  31.8 12.8 %copy-start.5 = (s32[1,64]{1,0:T(1,128)S(1)}, s32[1,64]{1,0:T(1,128)}, u32[]{:S(2)}) copy-start(s32[1,64]{1,0:T(1,128)} %param.16) | copy-start | bytes 772
  32.4 0.7 copy-start.3
  33.8 10.8 %all-to-all-start.1 = ((bf16[4,16,512]{2,1,0:T(8,128)(2,1)}), bf16[4,16,512]{2,1,0:T(8,128)(2,1)S(1)}, u32[]{:S(2)}, u32[]{:S(2)}) async-start(bf16[4,16,512]{2,1,0:T(8,128)(2,1)} %bitcast.10), calls=%async_computation.1 | async-start | bytes 131072 | tf_op jit(solution)/shard_map/all_to_all | solution.py:21
  49.8 9.7 %all-to-all-start.2 = ((bf16[4,16,512]{2,1,0:T(8,128)(2,1)}), bf16[4,16,512]{2,1,0:T(8,128)(2,1)}, u32[]{:S(2)}, u32[]{:S(2)}) async-start(bf16[4,16,512]{2,1,0:T(8,128)(2,1)} %broadcast_select_fusion), calls=%async_computation.2 | async-start | bytes 131072 | tf_op jit(solution)/shard_map/all_to_all | solution.py:12
  53.7 65.5 %reduce-scatter.2.cloned.1.call-start = ((), (), s32[]{:S(2)}) async-start(), calls=%async_computation.5 | async-start | bytes 5898240 | tf_op jit(solution)/shard_map/reduce_scatter | solution.py:86
  59.5 1.7 copy-start.2
  119.2 16.5 %collective-permute-start = (f32[5,64,512]{2,1,0:T(8,128)}, f32[5,64,512]{2,1,0:T(8,128)S(1)}, u32[]{:S(2)}, u32[]{:S(2)}) collective-permute-start(f32[5,64,512]{2,1,0:T(8,128)} %reduce-scatter.2.cloned.1.call-done), channel_id=1, source_target_pairs={{0,8},{8,0},{16,24},{24,16},{1,9},{9,1},{17,25},{25,17},{2,10},{10... | collective-permute-start | bytes 1966088 | tf_op jit(solution)/shard_map/ppermute | solution.py:89
  137.0 34.1 %collective-permute-start.1 = (f32[5,64,512]{2,1,0:T(8,128)S(1)}, f32[5,64,512]{2,1,0:T(8,128)}, u32[]{:S(2)}, u32[]{:S(2)}) collective-permute-start(f32[5,64,512]{2,1,0:T(8,128)S(1)} %add.75), channel_id=1, source_target_pairs={{0,16},{8,24},{16,0},{24,8},{1,17},{9,25},{17,1},{25,9},{2,18},{10... | collective-permute-start | bytes 1966088 | tf_op jit(solution)/shard_map/ppermute | solution.py:89
Sparse Core Ops, SparseCore 0:
  64.2 54.9 reduce-scatter.1
